TPU v7x, 32 devices: a whole 2x2x4 slice. The times are simulated.
32 devices in a mesh: dp: 4 (over y, x), fsdp: 8 (over z, core).
Axes of the slice: x: 2, y: 2, z: 4, core: 2. Of those that a mesh axis runs over, the one named last changes fastest.
Arguments:
- hidden_in: bfloat16 [32, 8192], P(('dp', 'fsdp')), may hold values from -6 to 6
- lengths: int32 [32], P(('dp', 'fsdp')), may hold values from 1 to 511
- key_cache: bfloat16 [32, 512, 1024], P(('dp', 'fsdp')), may hold values from -68 to 68
- value_cache: bfloat16 [32, 512, 1024], P(('dp', 'fsdp')), may hold values from -6 to 6
- attn_gain: bfloat16 [8192], replicated, may hold values from 0.5 to 1.5
- w_qkv: bfloat16 [8192, 10240], P('fsdp', 'dp'), may hold values from -0.0625 to 0.0625
- w_out: bfloat16 [8192, 8192], P('fsdp', 'dp'), may hold values from -0.5 to 0.5
- mlp_gain: bfloat16 [8192], replicated, may hold values from 0.5 to 1.5
- w_gate: bfloat16 [8192, 28672], P('dp', 'fsdp'), may hold values from -0.0625 to 0.0625
- w_up: bfloat16 [8192, 28672], P('dp', 'fsdp'), may hold values from -0.0625 to 0.0625
- w_down: bfloat16 [28672, 8192], P('fsdp', 'dp'), may hold values from -0.03125 to 0.03125
Outputs:
- hidden_out: bfloat16 [32, 8192], P(('dp', 'fsdp'))
- new_keys: bfloat16 [32, 1024], P(('dp', 'fsdp'))
- new_values: bfloat16 [32, 1024], P(('dp', 'fsdp'))
Inputs may be any that keep to these rules, and one draw needn't show every extreme that they name: Each sequence's number of cached positions; its new token takes position lengths.
All inputs are finite; a program needn't handle non-finite values.
Results may differ from a plain program's by a relative error of at most 0.012.
The roundings to bfloat16 on the way count: a program that leaves them out, or rounds other values in their place, can miss the bound.
Values may be sent and summed in bfloat16 or wider, within the bound.
A program may use at most 128 MiB of HBM per device.

v0:
```python
import jax
import jax.numpy as jnp
from jax import lax
from jax.sharding import PartitionSpec as P

HEADS = 64
KV_HEADS = 8
HD = 128
rope_base = 500000.0
norm_eps = 1e-05


def rms_scale(values, gain_row):
    mean_square = jnp.mean(values * values, axis=-1, keepdims=True)
    return values * lax.rsqrt(mean_square + norm_eps) * gain_row.astype(jnp.float32)


def rotate(values, positions):
    half_dim = values.shape[-1] // 2
    frequency = rope_base ** (-2.0 * jnp.arange(half_dim, dtype=jnp.float32) / values.shape[-1])
    angles = positions.astype(jnp.float32)[:, None] * frequency[None, :]
    cosine = jnp.cos(angles)[:, None, :]
    sine_wave = jnp.sin(angles)[:, None, :]
    lower_half = values[..., :half_dim]
    upper_half = values[..., half_dim:]
    return jnp.concatenate(
        [
            lower_half * cosine - upper_half * sine_wave,
            upper_half * cosine + lower_half * sine_wave,
        ],
        axis=-1,
    )


def attend(queries, new_keys, new_values, key_cache, value_cache, lengths):
    seq_count, context, kv_width = key_cache.shape
    kv_heads = new_keys.shape[1]
    head_dim = new_keys.shape[2]
    score_scale = head_dim ** (-0.5)
    key_rows = key_cache.reshape(seq_count, context, kv_heads, head_dim)
    value_rows = value_cache.reshape(seq_count, context, kv_heads, head_dim)
    grouped = queries.reshape(seq_count, kv_heads, -1, head_dim)
    scores = (
        jnp.einsum("skgd,sckd->skgc", grouped, key_rows, preferred_element_type=jnp.float32)
        * score_scale
    )
    is_valid = (
        jnp.arange(context, dtype=jnp.int32)[None, None, None, :] < lengths[:, None, None, None]
    )
    scores = jnp.where(is_valid, scores, -1e30)
    own_score = (
        jnp.einsum("skgd,skd->skg", grouped, new_keys, preferred_element_type=jnp.float32)
        * score_scale
    )
    row_max = jnp.maximum(jnp.max(scores, axis=-1), own_score)
    weights = jnp.exp(scores - row_max[..., None])
    own_weight = jnp.exp(own_score - row_max)
    denom_sum = jnp.sum(weights, axis=-1) + own_weight
    probability = (weights / denom_sum[..., None]).astype(jnp.bfloat16)
    own_prob = (own_weight / denom_sum).astype(jnp.bfloat16)
    mixed = jnp.einsum(
        "skgc,sckd->skgd", probability, value_rows, preferred_element_type=jnp.float32
    )
    mixed = (
        mixed
        + own_prob.astype(jnp.float32)[..., None] * new_values.astype(jnp.float32)[:, :, None, :]
    )
    return mixed.astype(jnp.bfloat16).reshape(seq_count, -1)


def quarter_split(values, dp_size, fsdp_size):
    seq_count = values.shape[0]
    return values.reshape(seq_count, fsdp_size, dp_size, -1)


def quarter_join(moved, dp_size):
    return moved.reshape(dp_size, moved.shape[0] // dp_size, -1)[None]


def on_device(
    hidden_in,
    lengths,
    key_cache,
    value_cache,
    attn_gain,
    w_qkv,
    w_out,
    mlp_gain,
    w_gate,
    w_up,
    w_down,
):
    seq_count = hidden_in.shape[0]
    q_width = HEADS * HD
    kv_width = KV_HEADS * HD
    dp_size = lax.axis_size("dp")
    fsdp_size = lax.axis_size("fsdp")
    residual = hidden_in.astype(jnp.float32)
    normed = rms_scale(residual, attn_gain).astype(jnp.bfloat16)
    qkv_tile = lax.all_to_all(
        lax.all_to_all(w_qkv, "dp", split_axis=0, concat_axis=1, tiled=True),
        "fsdp",
        split_axis=1,
        concat_axis=0,
        tiled=True,
    )
    qkv_moved = lax.all_to_all(
        quarter_split(normed, dp_size, fsdp_size), "dp", split_axis=2, concat_axis=0, tiled=True
    )
    qkv_in = quarter_join(qkv_moved, dp_size)
    qkv_parts = jnp.einsum(
        "fpsk,kn->fpsn",
        lax.all_gather(qkv_in, "fsdp", axis=0, tiled=True),
        qkv_tile,
        preferred_element_type=jnp.float32,
    )
    qkv_share = lax.psum_scatter(qkv_parts, "dp", scatter_dimension=1, tiled=True)
    projected = lax.all_to_all(qkv_share, "fsdp", split_axis=0, concat_axis=3, tiled=True)[0, 0]
    queries = rotate(projected[:, :q_width].reshape(seq_count, HEADS, HD), lengths).astype(
        jnp.bfloat16
    )
    new_keys = rotate(
        projected[:, q_width : q_width + kv_width].reshape(seq_count, KV_HEADS, HD), lengths
    ).astype(jnp.bfloat16)
    new_values = projected[:, q_width + kv_width :].astype(jnp.bfloat16)
    mixed = attend(
        queries,
        new_keys,
        new_values.reshape(seq_count, KV_HEADS, HD),
        key_cache,
        value_cache,
        lengths,
    )
    out_tile = lax.all_to_all(
        lax.all_to_all(w_out, "dp", split_axis=0, concat_axis=1, tiled=True),
        "fsdp",
        split_axis=1,
        concat_axis=0,
        tiled=True,
    )
    out_moved = lax.all_to_all(
        quarter_split(mixed, dp_size, fsdp_size), "dp", split_axis=2, concat_axis=0, tiled=True
    )
    out_in = quarter_join(out_moved, dp_size)
    out_parts = jnp.einsum(
        "fpsk,kn->fpsn",
        lax.all_gather(out_in, "fsdp", axis=0, tiled=True),
        out_tile,
        preferred_element_type=jnp.float32,
    )
    out_share = lax.psum_scatter(out_parts, "dp", scatter_dimension=1, tiled=True)
    attn_sum = lax.all_to_all(out_share, "fsdp", split_axis=0, concat_axis=3, tiled=True)[0, 0]
    residual_mid = residual + attn_sum
    normed_mid = rms_scale(residual_mid, mlp_gain).astype(jnp.bfloat16)
    mlp_in = lax.all_to_all(normed_mid[None], "dp", split_axis=2, concat_axis=0, tiled=True)
    pieces = lax.all_gather(mlp_in[None], "fsdp", axis=0, tiled=True)
    gate_part = jnp.einsum("fask,kn->fasn", pieces, w_gate, preferred_element_type=jnp.float32)
    up_part = jnp.einsum("fask,kn->fasn", pieces, w_up, preferred_element_type=jnp.float32)
    partials = jnp.stack([gate_part, up_part], axis=3)
    summed = lax.psum(partials.astype(jnp.bfloat16), "dp").astype(jnp.float32)
    activated = (jax.nn.silu(summed[:, :, :, 0]) * summed[:, :, :, 1]).astype(jnp.bfloat16)
    reduced_down = lax.psum_scatter(
        jnp.einsum("fask,kn->fasn", activated, w_down, preferred_element_type=jnp.float32),
        "fsdp",
        scatter_dimension=0,
        tiled=True,
    )
    down_sum = lax.all_to_all(
        reduced_down.astype(jnp.bfloat16), "dp", split_axis=1, concat_axis=3, tiled=True
    ).astype(reduced_down.dtype)[0, 0]
    hidden_out = (residual_mid + down_sum).astype(jnp.bfloat16)
    return (hidden_out, new_keys.reshape(seq_count, kv_width), new_values)


def solution(mesh):
    in_specs = (
        P(("dp", "fsdp"), None),
        P(("dp", "fsdp")),
        P(("dp", "fsdp"), None, None),
        P(("dp", "fsdp"), None, None),
        P(),
        P("fsdp", "dp"),
        P("fsdp", "dp"),
        P(),
        P("dp", "fsdp"),
        P("dp", "fsdp"),
        P("fsdp", "dp"),
    )
    out_specs = (P(("dp", "fsdp"), None), P(("dp", "fsdp"), None), P(("dp", "fsdp"), None))
    return jax.shard_map(
        on_device, mesh=mesh, in_specs=in_specs, out_specs=out_specs, check_vma=False
    )
```

profile of v0, /device:TPU:0, one launch (start us, length us, event | category | flops | bytes accessed | tf_op | source)
XLA Modules:
  0.0 717.8 jit_solution(7056581813542173455)
XLA Ops:
  7.2 5.3 all-to-all-start.1
  14.6 57.9 %all-to-all-done.1 = bf16[4,256,2560]{2,1,0:T(8,128)(2,1)} async-done(((bf16[4,256,2560]{2,1,0:T(8,128)(2,1)}), bf16[4,256,2560]{2,1,0:T(8,128)(2,1)}, u32[]{:S(2)}, u32[]{:S(2)}) %all-to-all-start.1) | async-done | bytes 5242912 | tf_op jit(solution)/shard_map/all_to_all | solution.py:101
  75.8 8.0 %copy.52 = bf16[256,4,2560]{0,2,1:T(8,128)(2,1)} copy(bf16[256,4,2560]{2,0,1:T(8,128)(2,1)} %bitcast.6) | data formatting | bytes 10485760 | tf_op jit(solution)/shard_map/all_to_all | solution.py:101
  83.8 121.6 %all_to_all.136 = bf16[256,8,1280]{0,2,1:T(8,128)(2,1)} all-to-all(bf16[256,8,1280]{0,2,1:T(8,128)(2,1)} %bitcast.137), channel_id=1, replica_groups=mesh['dp'=4,'fsdp'=8] {'fsdp'}, dimensions={1} | all-to-all | bytes 10485760 | tf_op jit(solution)/shard_map/all_to_all | solution.py:100
  210.4 14.0 %all_gather.9 = bf16[8,4,1,2048]{3,1,2,0:T(4,128)(2,1)S(1)} all-gather(bf16[1,4,1,2048]{3,1,2,0:T(4,128)(2,1)S(1)} %broadcast_in_dim_reshape.6), channel_id=1, replica_groups=mesh['dp'=4,'fsdp'=8] {'fsdp'}, dimensions={0}, use_global_device_ids=true | all-gather | bytes 147456 | tf_op jit(solution)/shard_map/all_gather | solution.py:113
  224.3 7.8 %copy.53 = bf16[8,256,1280]{2,1,0:T(8,128)(2,1)} copy(bf16[8,256,1280]{1,2,0:T(8,128)(2,1)} %bitcast.136) | data formatting | bytes 10485760 | tf_op jit(solution)/shard_map/all_to_all | solution.py:100
  236.3 32.0 %reduce-scatter.9.cloned.1.call-done = f32[8,1,1,1280]{3,0,1,2:T(8,128)} async-done(((f32[8,4,1,1280]{3,0,1,2:T(8,128)}), f32[8,1,1,1280]{3,0,1,2:T(8,128)}) %reduce-scatter.9.cloned.1.call-update) | async-done | bytes 40976
  274.3 6.2 copy.59
  289.8 90.0 %all-to-all-done.6 = bf16[256,8,1024]{0,2,1:T(8,128)(2,1)} async-done(((bf16[256,8,1024]{0,2,1:T(8,128)(2,1)}), bf16[256,8,1024]{0,2,1:T(8,128)(2,1)}, u32[]{:S(2)}, u32[]{:S(2)}) %all-to-all-start.6) | async-done | bytes 4194336 | tf_op jit(solution)/shard_map/all_to_all | solution.py:134
  383.1 6.5 copy.60
  389.6 14.0 %all_gather.10 = bf16[8,4,1,2048]{3,1,2,0:T(4,128)(2,1)S(1)} all-gather(bf16[1,4,1,2048]{3,1,2,0:T(4,128)(2,1)S(1)} %broadcast_in_dim_reshape.7), channel_id=1, replica_groups=mesh['dp'=4,'fsdp'=8] {'fsdp'}, dimensions={0}, use_global_device_ids=true | all-gather | bytes 147456 | tf_op jit(solution)/shard_map/all_gather | solution.py:147
  407.2 23.6 %reduce-scatter.11.cloned.1.call-done = f32[8,1,1,1024]{3,0,1,2:T(8,128)} async-done(((f32[8,4,1,1024]{3,0,1,2:T(8,128)}), f32[8,1,1,1024]{3,0,1,2:T(8,128)}) %reduce-scatter.11.cloned.1.call-update) | async-done | bytes 32784
  437.1 5.5 all-to-all-done.7
  444.0 6.8 copy.62
  451.3 62.6 %reduce.10 = bf16[8192]{0:T(1024)(128)(2,1)S(1)} reduce(bf16[8192,1,1]{2,1,0:T(2,128)(2,1)} %bitcast.139, bf16[]{:T(256)} %broadcast.87), dimensions={1,2}, to_apply=%bitcast.123.reduce_sub_computation | reduce | bytes 32770
  513.9 7.3 %all_to_all.137 = bf16[4,2,1024]{2,1,0:T(2,128)(2,1)S(1)} all-to-all(bf16[4,2,1024]{2,1,0:T(2,128)(2,1)S(1)} %reshape.331), channel_id=1, replica_groups=mesh['dp'=4,'fsdp'=8] {'dp'}, dimensions={0} | all-to-all | bytes 32768 | tf_op jit(solution)/shard_map/all_to_all | solution.py:155
  521.2 5.6 reshape.332
  526.8 62.0 %bitcast_reduce_fusion = bf16[8192]{0:T(1024)(128)(2,1)S(1)} fusion(bf16[8192,1,1]{2,1,0:T(2,128)(2,1)} %reshape.332), kind=kLoop, calls=%fused_computation.73 | loop fusion | bytes 32768 | tf_op jit(solution)/shard_map/all_to_all | solution.py:155
  588.8 14.2 %all_gather.11 = bf16[8,4,1,2048]{3,1,2,0:T(4,128)(2,1)S(1)} all-gather(bf16[1,4,1,2048]{3,1,2,0:T(4,128)(2,1)S(1)} %broadcast_in_dim.53), channel_id=1, replica_groups=mesh['dp'=4,'fsdp'=8] {'fsdp'}, dimensions={0}, use_global_device_ids=true | all-gather | bytes 147456 | tf_op jit(solution)/shard_map/all_gather | solution.py:156
  603.0 7.6 %fusion.12 = bf16[8,4,1,1,3584]{4,0,1,3,2:T(8,128)(2,1)S(1)} fusion(bf16[2048,3584]{1,0:T(8,128)(2,1)} %param.20, bf16[8,4,1,2048]{3,1,2,0:T(4,128)(2,1)S(1)} %all_gather.11), kind=kOutput, calls=%fused_computation.8 | convolution fusion | flops 469876736 | bytes 15040512 | tf_op jit(solution)/shard_map/fask,kn->fasn/dot_general | solution.py:158
  610.6 7.7 %fusion.15 = bf16[8,4,1,1,3584]{4,0,1,3,2:T(8,128)(2,1)S(1)} fusion(bf16[2048,3584]{1,0:T(8,128)(2,1)} %param.19, bf16[8,4,1,2048]{3,1,2,0:T(4,128)(2,1)S(1)} %all_gather.11), kind=kOutput, calls=%fused_computation.9 | convolution fusion | flops 469876736 | bytes 15040512 | tf_op jit(solution)/shard_map/fask,kn->fasn/dot_general | solution.py:157
  619.8 40.7 %all-reduce.6.cloned.1.call-done = bf16[8,4,1,2,3584]{4,0,1,3,2:T(8,128)(2,1)} async-done(((bf16[8,4,1,2,3584]{4,0,1,3,2:T(8,128)(2,1)}), bf16[8,4,1,2,3584]{4,0,1,3,2:T(8,128)(2,1)}) %all-reduce.6.cloned.1.call-update) | async-done | bytes 458768 | tf_op jit(solution)/shard_map/psum | solution.py:160
  661.6 7.7 %fusion.18 = f32[8,4,1,2048]{3,0,1,2:T(8,128)S(1)} fusion(bf16[3584,2048]{1,0:T(8,128)(2,1)} %param.21, f32[8,4,1,2,3584]{4,0,1,3,2:T(8,128)S(1)} %convert_element_type.113), kind=kOutput, calls=%fused_computation.10 | convolution fusion | flops 470450176 | bytes 15859712 | tf_op jit(solution)/shard_map/fask,kn->fasn/dot_general | solution.py:163
  669.5 31.1 %all-reduce.7 = bf16[8,4,1,2048]{3,1,2,0:T(4,128)(2,1)S(1)} all-reduce(f32[8,4,1,2048]{3,1,2,0:T(4,128)S(1)} %copy.64), channel_id=4, replica_groups=mesh['dp'=4,'fsdp'=8] {'fsdp'}, use_global_device_ids=true, to_apply=%region_7.8.clone | all-reduce | flops 65536 | bytes 393216
  (77 shorter events, 56.0 us)
Async XLA Ops:
  7.2 5.4 copy-start.3
  7.2 5.4 copy-start.2
  7.2 65.4 %all-to-all-start.1 = ((bf16[4,256,2560]{2,1,0:T(8,128)(2,1)}), bf16[4,256,2560]{2,1,0:T(8,128)(2,1)}, u32[]{:S(2)}, u32[]{:S(2)}) async-start(bf16[4,256,2560]{2,1,0:T(8,128)(2,1)} %bitcast.140), calls=%async_computation.1 | async-start | bytes 10485760 | tf_op jit(solution)/shard_map/all_to_all | solution.py:101
  72.5 11.2 %all-to-all-start = ((bf16[1,8,4,256]{3,1,0,2:T(8,128)(2,1)}), bf16[1,8,4,256]{3,1,0,2:T(8,128)(2,1)S(1)}, u32[]{:S(2)}, u32[]{:S(2)}) async-start(bf16[1,8,4,256]{3,1,0,2:T(8,128)(2,1)} %copy.50), calls=%async_computation | async-start | bytes 32768 | tf_op jit(solution)/shard_map/all_to_all | solution.py:107
  205.4 64.3 %all-to-all-start.5 = ((bf16[4,256,2048]{2,1,0:T(8,128)(2,1)}), bf16[4,256,2048]{2,1,0:T(8,128)(2,1)}, u32[]{:S(2)}, u32[]{:S(2)}) async-start(bf16[4,256,2048]{2,1,0:T(8,128)(2,1)} %bitcast.141), calls=%async_computation.5 | async-start | bytes 8388608 | tf_op jit(solution)/shard_map/all_to_all | solution.py:135
  210.3 58.0 %reduce-scatter.9.cloned.1.call-start = ((), (), s32[]{:S(2)}) async-start(), calls=%async_computation.13 | async-start | bytes 204800
  269.7 10.8 %all-to-all-start.3 = ((f32[8,1,1,1280]{3,1,2,0:T(1,128)}), f32[8,1,1,1280]{3,1,2,0:T(1,128)S(1)}, u32[]{:S(2)}, u32[]{:S(2)}) async-start(f32[8,1,1,1280]{3,1,2,0:T(1,128)} %copy.54), calls=%async_computation.3 | async-start | bytes 81920 | tf_op jit(solution)/shard_map/all_to_all | solution.py:118
  280.5 5.9 copy-start
  280.5 6.2 copy-start.1
  280.5 99.3 %all-to-all-start.6 = ((bf16[256,8,1024]{0,2,1:T(8,128)(2,1)}), bf16[256,8,1024]{0,2,1:T(8,128)(2,1)}, u32[]{:S(2)}, u32[]{:S(2)}) async-start(bf16[256,8,1024]{0,2,1:T(8,128)(2,1)} %bitcast.138), calls=%async_computation.6 | async-start | bytes 8388608 | tf_op jit(solution)/shard_map/all_to_all | solution.py:134
  379.8 9.8 %all-to-all-start.4 = ((bf16[1,8,4,256]{3,1,0,2:T(8,128)(2,1)}), bf16[1,8,4,256]{3,1,0,2:T(8,128)(2,1)S(1)}, u32[]{:S(2)}, u32[]{:S(2)}) async-start(bf16[1,8,4,256]{3,1,0,2:T(8,128)(2,1)} %copy.57), calls=%async_computation.4 | async-start | bytes 32768 | tf_op jit(solution)/shard_map/all_to_all | solution.py:141
  383.1 47.8 %reduce-scatter.11.cloned.1.call-start = ((), (), s32[]{:S(2)}) async-start(), calls=%async_computation.14 | async-start | bytes 163840
  389.6 47.5 %copy-start.4 = (bf16[8192]{0:T(1024)(128)(2,1)S(1)}, bf16[8192]{0:T(1024)(128)(2,1)}, u32[]{:S(2)}) copy-start(bf16[8192]{0:T(1024)(128)(2,1)} %param.18) | copy-start | bytes 49156
  432.2 10.3 %all-to-all-start.7 = ((f32[8,1,1,1024]{3,1,2,0:T(1,128)}), f32[8,1,1,1024]{3,1,2,0:T(1,128)S(1)}, u32[]{:S(2)}, u32[]{:S(2)}) async-start(f32[8,1,1,1024]{3,1,2,0:T(1,128)} %copy.61), calls=%async_computation.7 | async-start | bytes 65536 | tf_op jit(solution)/shard_map/all_to_all | solution.py:152
  436.8 223.7 %all-reduce.6.cloned.1.call-start = ((), (), s32[]{:S(2)}) async-start(), calls=%async_computation.12 | async-start | bytes 917504 | tf_op jit(solution)/shard_map/psum | solution.py:160
  610.6 8.5 %copy-start.5 = (u32[32]{0:T(128)S(1)}, u32[32]{0:T(128)}, u32[]{:S(2)}) copy-start(u32[32]{0:T(128)} %constant.44) | copy-start | bytes 388
  702.6 7.9 %all-to-all-start.9 = ((bf16[4,2,1024]{2,1,0:T(2,128)(2,1)}), bf16[4,2,1024]{2,1,0:T(2,128)(2,1)S(1)}, u32[]{:S(2)}, u32[]{:S(2)}) async-start(bf16[4,2,1024]{2,1,0:T(2,128)(2,1)} %reshape.333), calls=%async_computation.9 | async-start | bytes 32768 | tf_op jit(solution)/shard_map/all_to_all | solution.py:168
Sparse Core Ops, SparseCore 0:
  236.4 31.7 reduce-scatter.8
  407.3 23.4 reduce-scatter.10
  619.3 41.1 all-reduce.5
where the time goes:
time: 720 us; the launch traced here: 718 us
  waiting for transfers between devices  254 us (35%)
  blocking collectives  202 us (28%)
  local copies, waits for them, and re-layouts  111 us (15%)
  other arithmetic  68.6 us (10%)
  starting transfers between devices  34.7 us (5%)
  matrix products  31.7 us (4%)
  between operations  16 us (2%)
    all_to_all x1, blocking collectives, on_device(): lax.all_to_all(lax.all_to_all(w_qkv, 'dp', split_axis=0, concat_axis=1, t...  122 us
    all_to_all x1, waiting for transfers between devices, on_device(): lax.all_to_all(lax.all_to_all(w_out, 'dp', split_axis=0, concat_axis=1, t...  90 us
    unnamed x3, other arithmetic  63.4 us
    all_to_all x1, local copies, waits for them, and re-layouts, on_device(): lax.all_to_all(normed_mid[None], 'dp', split_axis=2, concat_axis=0, tiled...  62 us
    all_to_all x1, waiting for transfers between devices, on_device(): lax.all_to_all(w_qkv, 'dp', split_axis=0, concat_axis=1, tiled=True)  57.9 us
    unnamed x5, waiting for transfers between devices  55.7 us
    psum x1, waiting for transfers between devices, on_device(): summed = lax.psum(partials.astype(jnp.bfloat16), 'dp').astype(jnp.float32)  40.7 us
    unnamed x1, blocking collectives  31.1 us
  transfers between devices with their start and end apart: 11, of which 7 were waited for; matrix products, arithmetic and copies ran while one was open for 6% of the time, Pallas kernels for 0%

commit v1 on v0

--- a/solution.py
+++ b/solution.py
@@ -8,6 +8,13 @@
 HD = 128
 rope_base = 500000.0
 norm_eps = 1e-05
+
+
+def exchange_blocks(value, axis, split, join):
+    count = lax.axis_size(axis)
+    blocks = jnp.stack(jnp.split(value, count, axis=split), axis=0)
+    blocks = lax.all_to_all(blocks, axis, split_axis=0, concat_axis=0)
+    return jnp.concatenate(blocks, axis=join)
 
 
 def rms_scale(values, gain_row):
@@ -131,12 +138,8 @@
         value_cache,
         lengths,
     )
-    out_tile = lax.all_to_all(
-        lax.all_to_all(w_out, "dp", split_axis=0, concat_axis=1, tiled=True),
-        "fsdp",
-        split_axis=1,
-        concat_axis=0,
-        tiled=True,
+    out_tile = exchange_blocks(
+        lax.all_to_all(w_out, "dp", split_axis=0, concat_axis=1, tiled=True), "fsdp", 1, 0
     )
     out_moved = lax.all_to_all(
         quarter_split(mixed, dp_size, fsdp_size), "dp", split_axis=2, concat_axis=0, tiled=True

time: 720 us -> 747 us (1.038)
  blocking collectives: 202 us -> 348 us
  waiting for transfers between devices: 254 us -> 136 us
    all_to_all x3 -> x2, waiting for transfers between devices: 148 us -> 0.01 us  [the longest x1 0.01 us: on_device(): lax.all_to_all(lax.all_to_all(w_qkv, 'dp', split_axis=0, concat_axis=1, t...]
    all_gather x1, blocking collectives: 14 us -> 121 us  [on_device(): lax.all_gather(qkv_in, 'fsdp', axis=0, tiled=True)]
    all_gather x1, blocking collectives: 14 us -> 100 us  [on_device(): lax.all_gather(out_in, 'fsdp', axis=0, tiled=True)]
    all_to_all x1 -> x2, blocking collectives: 122 us -> 73.7 us  [the longest x1 64 us: on_device(): lax.all_to_all(w_qkv, 'dp', split_axis=0, concat_axis=1, tiled=True)]
    all_to_all x1, waiting for transfers between devices: 0.01 us -> 36.9 us  [on_device(): lax.all_to_all(w_out, 'dp', split_axis=0, concat_axis=1, tiled=True)]
    unnamed x5, waiting for transfers between devices: 55.7 us -> 42.6 us
    unnamed x21 -> x28, local copies, waits for them, and re-layouts: 8.48 us -> 18.1 us
  transfers between devices with their start and end apart: 11 -> 10, of which waited for: 7 -> 8; matrix products, arithmetic and copies ran while one was open for 6% -> 3% of each run, Pallas kernels for 0% -> 0%
where the time goes in v1:
time: 747 us; the launch traced here: 745 us
  blocking collectives  348 us (47%)
  waiting for transfers between devices  136 us (18%)
  local copies, waits for them, and re-layouts  111 us (15%)
  other arithmetic  70.9 us (9%)
  matrix products  31.7 us (4%)
  starting transfers between devices  30.4 us (4%)
  between operations  16 us (2%)
    all_gather x1, blocking collectives, on_device(): lax.all_gather(qkv_in, 'fsdp', axis=0, tiled=True)  121 us
    all_gather x1, blocking collectives, on_device(): lax.all_gather(out_in, 'fsdp', axis=0, tiled=True)  100 us
    all_to_all x1, blocking collectives, on_device(): lax.all_to_all(w_qkv, 'dp', split_axis=0, concat_axis=1, tiled=True)  64 us
    unnamed x3, other arithmetic  63.4 us
    all_to_all x1, local copies, waits for them, and re-layouts, on_device(): lax.all_to_all(normed_mid[None], 'dp', split_axis=2, concat_axis=0, tiled...  62 us
    unnamed x5, waiting for transfers between devices  42.6 us
    psum x1, waiting for transfers between devices, on_device(): summed = lax.psum(partials.astype(jnp.bfloat16), 'dp').astype(jnp.float32)  40.7 us
    all_to_all x1, waiting for transfers between devices, on_device(): lax.all_to_all(w_out, 'dp', split_axis=0, concat_axis=1, tiled=True)  36.9 us
  transfers between devices with their start and end apart: 10, of which 8 were waited for; matrix products, arithmetic and copies ran while one was open for 3% of the time, Pallas kernels for 0%

profile of v1, /device:TPU:0, one launch (start us, length us, event | category | flops | bytes accessed | tf_op | source)
XLA Modules:
  0.0 744.8 jit_solution(15578926886328867678)
XLA Ops:
  10.9 9.7 %all_to_all.125 = bf16[1,8,4,256]{3,1,0,2:T(8,128)(2,1)S(1)} all-to-all(bf16[1,8,4,256]{3,1,0,2:T(8,128)(2,1)S(1)} %copy.49), channel_id=1, replica_groups=mesh['dp'=4,'fsdp'=8] {'dp'}, dimensions={2} | all-to-all | bytes 32768 | tf_op jit(solution)/shard_map/all_to_all | solution.py:114
  20.6 64.0 %all_to_all.126 = bf16[4,256,2560]{2,1,0:T(8,128)(2,1)} all-to-all(bf16[4,256,2560]{2,1,0:T(8,128)(2,1)} %bitcast.178), channel_id=1, replica_groups=mesh['dp'=4,'fsdp'=8] {'dp'}, dimensions={0} | all-to-all | bytes 10485760 | tf_op jit(solution)/shard_map/all_to_all | solution.py:108
  84.6 4.8 all-to-all-start.5
  89.5 7.9 %copy.51 = bf16[256,4,2560]{0,2,1:T(8,128)(2,1)} copy(bf16[256,4,2560]{2,0,1:T(8,128)(2,1)} %bitcast.168) | data formatting | bytes 10485760 | tf_op jit(solution)/shard_map/all_to_all | solution.py:108
  97.4 36.9 %all-to-all-done.5 = bf16[4,256,2048]{2,1,0:T(8,128)(2,1)} async-done(((bf16[4,256,2048]{2,1,0:T(8,128)(2,1)}), bf16[4,256,2048]{2,1,0:T(8,128)(2,1)}, u32[]{:S(2)}, u32[]{:S(2)}) %all-to-all-start.5) | async-done | bytes 4194336 | tf_op jit(solution)/shard_map/all_to_all | solution.py:142
  134.3 5.0 all-to-all-start.2
  140.7 121.5 %all_gather.9 = bf16[8,4,1,2048]{3,1,2,0:T(4,128)(2,1)S(1)} all-gather(bf16[1,4,1,2048]{3,1,2,0:T(4,128)(2,1)S(1)} %broadcast_in_dim_reshape.6), channel_id=1, replica_groups=mesh['dp'=4,'fsdp'=8] {'fsdp'}, dimensions={0}, use_global_device_ids=true | all-gather | bytes 147456 | tf_op jit(solution)/shard_map/all_gather | solution.py:120
  268.7 7.8 %copy.52 = bf16[8,256,1280]{2,1,0:T(8,128)(2,1)} copy(bf16[8,256,1280]{1,2,0:T(8,128)(2,1)} %bitcast.8) | data formatting | bytes 10485760 | tf_op jit(solution)/shard_map/all_to_all | solution.py:107
  284.4 19.9 %reduce-scatter.9.cloned.1.call-done = f32[8,1,1,1280]{3,0,1,2:T(8,128)} async-done(((f32[8,4,1,1280]{3,0,1,2:T(8,128)}), f32[8,1,1,1280]{3,0,1,2:T(8,128)}) %reduce-scatter.9.cloned.1.call-update) | async-done | bytes 40976
  305.7 4.6 all-to-all-start.3
  331.4 100.1 %all_gather.10 = bf16[8,4,1,2048]{3,1,2,0:T(4,128)(2,1)S(1)} all-gather(bf16[1,4,1,2048]{3,1,2,0:T(4,128)(2,1)S(1)} %broadcast_in_dim_reshape.7), channel_id=1, replica_groups=mesh['dp'=4,'fsdp'=8] {'fsdp'}, dimensions={0}, use_global_device_ids=true | all-gather | bytes 147456 | tf_op jit(solution)/shard_map/all_gather | solution.py:150
  435.1 22.7 %reduce-scatter.11.cloned.1.call-done = f32[8,1,1,1024]{3,0,1,2:T(8,128)} async-done(((f32[8,4,1,1024]{3,0,1,2:T(8,128)}), f32[8,1,1,1024]{3,0,1,2:T(8,128)}) %reduce-scatter.11.cloned.1.call-update) | async-done | bytes 32784
  464.1 5.5 all-to-all-done.7
  471.0 6.8 copy.60
  478.3 62.6 %reduce.10 = bf16[8192]{0:T(1024)(128)(2,1)S(1)} reduce(bf16[8192,1,1]{2,1,0:T(2,128)(2,1)} %bitcast.177, bf16[]{:T(256)} %broadcast.87), dimensions={1,2}, to_apply=%bitcast.155.reduce_sub_computation | reduce | bytes 32770
  541.0 7.3 all_to_all.127
  548.2 5.6 reshape.332
  553.8 62.0 %bitcast_reduce_fusion = bf16[8192]{0:T(1024)(128)(2,1)S(1)} fusion(bf16[8192,1,1]{2,1,0:T(2,128)(2,1)} %reshape.332), kind=kLoop, calls=%fused_computation.89 | loop fusion | bytes 32768 | tf_op jit(solution)/shard_map/all_to_all | solution.py:158
  615.8 14.2 %all_gather.11 = bf16[8,4,1,2048]{3,1,2,0:T(4,128)(2,1)S(1)} all-gather(bf16[1,4,1,2048]{3,1,2,0:T(4,128)(2,1)S(1)} %broadcast_in_dim.53), channel_id=1, replica_groups=mesh['dp'=4,'fsdp'=8] {'fsdp'}, dimensions={0}, use_global_device_ids=true | all-gather | bytes 147456 | tf_op jit(solution)/shard_map/all_gather | solution.py:159
  630.0 7.6 %fusion.12 = bf16[8,4,1,1,3584]{4,0,1,3,2:T(8,128)(2,1)S(1)} fusion(bf16[2048,3584]{1,0:T(8,128)(2,1)} %param.20, bf16[8,4,1,2048]{3,1,2,0:T(4,128)(2,1)S(1)} %all_gather.11), kind=kOutput, calls=%fused_computation.8 | convolution fusion | flops 469876736 | bytes 15040512 | tf_op jit(solution)/shard_map/fask,kn->fasn/dot_general | solution.py:161
  637.7 7.7 %fusion.15 = bf16[8,4,1,1,3584]{4,0,1,3,2:T(8,128)(2,1)S(1)} fusion(bf16[2048,3584]{1,0:T(8,128)(2,1)} %param.19, bf16[8,4,1,2048]{3,1,2,0:T(4,128)(2,1)S(1)} %all_gather.11), kind=kOutput, calls=%fused_computation.9 | convolution fusion | flops 469876736 | bytes 15040512 | tf_op jit(solution)/shard_map/fask,kn->fasn/dot_general | solution.py:160
  646.8 40.7 %all-reduce.6.cloned.1.call-done = bf16[8,4,1,2,3584]{4,0,1,3,2:T(8,128)(2,1)} async-done(((bf16[8,4,1,2,3584]{4,0,1,3,2:T(8,128)(2,1)}), bf16[8,4,1,2,3584]{4,0,1,3,2:T(8,128)(2,1)}) %all-reduce.6.cloned.1.call-update) | async-done | bytes 458768 | tf_op jit(solution)/shard_map/psum | solution.py:163
  688.6 7.7 %fusion.18 = f32[8,4,1,2048]{3,0,1,2:T(8,128)S(1)} fusion(bf16[3584,2048]{1,0:T(8,128)(2,1)} %param.21, f32[8,4,1,2,3584]{4,0,1,3,2:T(8,128)S(1)} %convert_element_type.113), kind=kOutput, calls=%fused_computation.10 | convolution fusion | flops 470450176 | bytes 15859712 | tf_op jit(solution)/shard_map/fask,kn->fasn/dot_general | solution.py:166
  696.5 31.1 %all-reduce.7 = bf16[8,4,1,2048]{3,1,2,0:T(4,128)(2,1)S(1)} all-reduce(f32[8,4,1,2048]{3,1,2,0:T(4,128)S(1)} %copy.62), channel_id=4, replica_groups=mesh['dp'=4,'fsdp'=8] {'fsdp'}, use_global_device_ids=true, to_apply=%region_7.8.clone | all-reduce | flops 65536 | bytes 393216
  (83 shorter events, 65.0 us)
Async XLA Ops:
  84.6 49.7 %all-to-all-start.5 = ((bf16[4,256,2048]{2,1,0:T(8,128)(2,1)}), bf16[4,256,2048]{2,1,0:T(8,128)(2,1)}, u32[]{:S(2)}, u32[]{:S(2)}) async-start(bf16[4,256,2048]{2,1,0:T(8,128)(2,1)} %bitcast.179), calls=%async_computation.5 | async-start | bytes 8388608 | tf_op jit(solution)/shard_map/all_to_all | solution.py:142
  134.3 5.7 copy-start.1
  134.3 6.0 copy-start.2
  134.3 134.3 %all-to-all-start.2 = ((bf16[256,8,1280]{0,2,1:T(8,128)(2,1)}), bf16[256,8,1280]{0,2,1:T(8,128)(2,1)}, u32[]{:S(2)}, u32[]{:S(2)}) async-start(bf16[256,8,1280]{0,2,1:T(8,128)(2,1)} %bitcast.167), calls=%async_computation.2 | async-start | bytes 10485760 | tf_op jit(solution)/shard_map/all_to_all | solution.py:107
  139.3 164.9 %reduce-scatter.9.cloned.1.call-start = ((), (), s32[]{:S(2)}) async-start(), calls=%async_computation.13 | async-start | bytes 204800
  264.7 3.1 copy-start
  305.7 10.4 %all-to-all-start.3 = ((f32[8,1,1,1280]{3,1,2,0:T(1,128)}), f32[8,1,1,1280]{3,1,2,0:T(1,128)S(1)}, u32[]{:S(2)}, u32[]{:S(2)}) async-start(f32[8,1,1,1280]{3,1,2,0:T(1,128)} %copy.53), calls=%async_computation.3 | async-start | bytes 81920 | tf_op jit(solution)/shard_map/all_to_all | solution.py:125
  318.8 7.9 %all-to-all-start.4 = ((bf16[1,8,4,256]{3,1,0,2:T(8,128)(2,1)}), bf16[1,8,4,256]{3,1,0,2:T(8,128)(2,1)S(1)}, u32[]{:S(2)}, u32[]{:S(2)}) async-start(bf16[1,8,4,256]{3,1,0,2:T(8,128)(2,1)} %copy.56), calls=%async_computation.4 | async-start | bytes 32768 | tf_op jit(solution)/shard_map/all_to_all | solution.py:144
  326.7 104.8 %all-to-all-start.6 = ((bf16[8,256,1024]{2,1,0:T(8,128)(2,1)}), bf16[8,256,1024]{2,1,0:T(8,128)(2,1)}, u32[]{:S(2)}, u32[]{:S(2)}) async-start(bf16[8,256,1024]{2,1,0:T(8,128)(2,1)} %fusion.25), calls=%async_computation.6 | async-start | bytes 8388608 | tf_op jit(solution)/shard_map/all_to_all | solution.py:16
  331.3 132.8 %copy-start.4 = (bf16[8192]{0:T(1024)(128)(2,1)S(1)}, bf16[8192]{0:T(1024)(128)(2,1)}, u32[]{:S(2)}) copy-start(bf16[8192]{0:T(1024)(128)(2,1)} %param.18) | copy-start | bytes 49156
  331.3 138.3 %copy-start.3 = (bf16[1,8192]{1,0:T(2,128)(2,1)S(1)}, bf16[1,8192]{1,0:T(2,128)(2,1)}, u32[]{:S(2)}) copy-start(bf16[1,8192]{1,0:T(2,128)(2,1)} %param.11) | copy-start | bytes 49156
  331.3 126.5 %reduce-scatter.11.cloned.1.call-start = ((), (), s32[]{:S(2)}) async-start(), calls=%async_computation.14 | async-start | bytes 163840
  459.3 10.3 %all-to-all-start.7 = ((f32[8,1,1,1024]{3,1,2,0:T(1,128)}), f32[8,1,1,1024]{3,1,2,0:T(1,128)S(1)}, u32[]{:S(2)}, u32[]{:S(2)}) async-start(f32[8,1,1,1024]{3,1,2,0:T(1,128)} %copy.59), calls=%async_computation.7 | async-start | bytes 65536 | tf_op jit(solution)/shard_map/all_to_all | solution.py:155
  463.8 223.7 %all-reduce.6.cloned.1.call-start = ((), (), s32[]{:S(2)}) async-start(), calls=%async_computation.12 | async-start | bytes 917504 | tf_op jit(solution)/shard_map/psum | solution.py:163
  637.6 8.5 %copy-start.5 = (u32[32]{0:T(128)S(1)}, u32[32]{0:T(128)}, u32[]{:S(2)}) copy-start(u32[32]{0:T(128)} %constant.44) | copy-start | bytes 388
  729.6 7.9 %all-to-all-start.9 = ((bf16[4,2,1024]{2,1,0:T(2,128)(2,1)}), bf16[4,2,1024]{2,1,0:T(2,128)(2,1)S(1)}, u32[]{:S(2)}, u32[]{:S(2)}) async-start(bf16[4,2,1024]{2,1,0:T(2,128)(2,1)} %reshape.333), calls=%async_computation.9 | async-start | bytes 32768 | tf_op jit(solution)/shard_map/all_to_all | solution.py:171
Sparse Core Ops, SparseCore 0:
  280.7 23.4 reduce-scatter.8
  435.2 22.5 reduce-scatter.10
  646.3 41.1 all-reduce.5
